TPU v7x, 256 devices: a whole 4x4x8 slice. The times are simulated.
256 devices in a mesh: seq: 8 (over z), tensor: 8 (over x, y_hi), dp: 4 (over y_lo, core).
Axes of the slice: x: 4, y: 4 (y_hi: 2, y_lo: 2; y = y_hi * 2 + y_lo), z: 8, core: 2. Of those that a mesh axis runs over, the one named last changes fastest.
Arguments:
- tokens: bfloat16 [4, 2048, 3072], P('dp', 'seq'), may hold values from -6 to 6
- cotangent: bfloat16 [4, 2048, 3072], P('dp', 'seq'), may hold values from -6 to 6
- qkv_weight: bfloat16 [3072, 3, 3072], P(('seq', 'dp'), None, 'tensor'), may hold values from -0.109375 to 0.109375
- out_weight: bfloat16 [3072, 3072], P(('seq', 'dp'), 'tensor'), may hold values from -0.109375 to 0.109375
Outputs:
- qkv_grad: float32 [3072, 3, 3072], P(('seq', 'dp'), None, 'tensor')
- out_grad: float32 [3072, 3072], P(('seq', 'dp'), 'tensor')
- branch_grad: bfloat16 [4, 2048, 3072], P('dp', 'seq', 'tensor')
All inputs are finite; a program needn't handle non-finite values.
Results may differ from a plain program's by a relative error of at most 0.025.
Values may be sent and summed in bfloat16 or wider, within the bound.
No kernel may reach another device: no remote copies, remote signals or barrier semaphores. Data moves between devices by JAX's collectives and lax.ppermute only.
A program may use at most 128 MiB of HBM per device.

v0:
```python
import jax
import jax.numpy as jnp
from jax import lax
from jax.sharding import PartitionSpec as P

HD = 128
epsilon = 1e-06


def sent_together(arrays, axis, dim, along):
    both = jnp.concatenate(arrays, axis=along)
    result, at, done = (lax.all_gather(both, axis, axis=dim, tiled=True), 0, [])
    for a in arrays:
        done.append(lax.slice_in_dim(result, at, at + a.shape[along], axis=along))
        at += a.shape[along]
    return tuple(done)


def split_up(shard, dim, size):
    before, after = (shard.shape[:dim], shard.shape[dim + 1 :])
    return jnp.moveaxis(shard.reshape(*before, size, -1, *after), dim, 0)


def summed_on_arrival(shard, axis, dim):
    size = lax.axis_size(axis)
    pieces = lax.all_to_all(split_up(shard, dim, size), axis, 0, 0, tiled=True)
    return jnp.sum(pieces.astype(jnp.float32), axis=0)


def copy_for_each(shard, axis):
    copies = jnp.broadcast_to(shard, (lax.axis_size(axis), *shard.shape))
    return lax.all_to_all(copies, axis, split_axis=0, concat_axis=0, tiled=True)


def taken_together(shard, axis):
    everything = copy_for_each(shard, axis)
    return jnp.sum(everything, axis=0)


def in_one(arrays, axis):
    ends = [0]
    for a in arrays:
        ends.append(ends[-1] + a.size)
    subtotal = taken_together(jnp.concatenate([a.ravel() for a in arrays]), axis)
    return tuple((subtotal[b:e].reshape(a.shape) for a, b, e in zip(arrays, ends, ends[1:])))


def normalize(values):
    average = jnp.mean(values, axis=-1, keepdims=True)
    centered = values - average
    inverse = lax.rsqrt(jnp.mean(centered * centered, axis=-1, keepdims=True) + epsilon)
    return (centered * inverse, inverse)


def normalize_back(gradient, normed, inverse):
    mean_grad = jnp.mean(gradient, axis=-1, keepdims=True)
    mean_both = jnp.mean(gradient * normed, axis=-1, keepdims=True)
    return (gradient - mean_grad - normed * mean_both) * inverse


def local(tokens, cotangent, qkv_weight, out_weight):
    row_count = tokens.shape[1]
    feature_count = tokens.shape[2]
    column_count = out_weight.shape[1]
    head_count = column_count // HD
    score_scale = HD ** (-0.5)
    own_rows = qkv_weight.shape[0]
    grad_rows = cotangent[0]
    normed, inverse = normalize(tokens[0].astype(jnp.float32))
    unit_low = normed.astype(jnp.bfloat16)
    flat_weight = qkv_weight.reshape(own_rows, 3 * column_count)
    piece_qkv, piece_out = sent_together((flat_weight, out_weight), ("seq", "dp"), 0, 1)
    piece_rows = piece_qkv.shape[0]
    left_rows = unit_low
    right_rows = grad_rows
    projected = jnp.dot(left_rows, piece_qkv, preferred_element_type=jnp.float32)
    attended_grad = jnp.dot(right_rows, piece_out, preferred_element_type=jnp.float32)
    full_qkv = piece_qkv
    projected, attended_grad, full_qkv = (projected, attended_grad, full_qkv)
    query_unit, query_inv = normalize(
        projected[:, :column_count].reshape(row_count, head_count, HD)
    )
    key_unit, key_inv = normalize(
        projected[:, column_count : 2 * column_count].reshape(row_count, head_count, HD)
    )
    query_low = query_unit.astype(jnp.bfloat16)
    key_value = jnp.stack(
        [
            key_unit.astype(jnp.bfloat16).reshape(row_count, column_count),
            projected[:, 2 * column_count :].astype(jnp.bfloat16),
        ]
    )
    grad_low = attended_grad.astype(jnp.bfloat16).reshape(row_count, head_count, HD)

    def scores_of(key_rows):
        piece_rows = key_rows.shape[0]
        return (
            jnp.einsum(
                "qhd,khd->hqk",
                query_low,
                key_rows.reshape(piece_rows, head_count, HD),
                preferred_element_type=jnp.float32,
            )
            * score_scale
        )

    every_pair = lax.all_gather(key_value, "seq", axis=1, tiled=True)
    piece_rows = every_pair.shape[1]
    exponent = jnp.exp(scores_of(every_pair[0]))
    add_exp_total = jnp.sum(exponent, axis=-1)
    weighted = jnp.einsum(
        "hqk,khd->qhd",
        exponent.astype(jnp.bfloat16),
        every_pair[1].reshape(piece_rows, head_count, HD),
        preferred_element_type=jnp.float32,
    )
    exp_total, weighted = (add_exp_total, weighted)
    attended_low = (weighted / exp_total.T[:, :, None]).astype(jnp.bfloat16)
    row_delta = jnp.sum(grad_low.astype(jnp.float32) * attended_low.astype(jnp.float32), axis=-1)
    piece_rows = every_pair.shape[1]
    key_rows = every_pair[0].reshape(piece_rows, head_count, HD)
    value_rows = every_pair[1].reshape(piece_rows, head_count, HD)
    probability = jnp.exp(scores_of(every_pair[0])) / exp_total[:, :, None]
    prob_grad = jnp.einsum("qhd,khd->hqk", grad_low, value_rows, preferred_element_type=jnp.float32)
    grad_score = (probability * (prob_grad - row_delta.T[:, :, None]) * score_scale).astype(
        jnp.bfloat16
    )
    query_part = jnp.einsum(
        "hqk,khd->qhd", grad_score, key_rows, preferred_element_type=jnp.float32
    )
    key_part = jnp.einsum("hqk,qhd->khd", grad_score, query_low, preferred_element_type=jnp.float32)
    value_part = jnp.einsum(
        "hqk,qhd->khd",
        probability.astype(jnp.bfloat16),
        grad_low,
        preferred_element_type=jnp.float32,
    )
    every_grad = jnp.stack(
        [key_part.reshape(piece_rows, column_count), value_part.reshape(piece_rows, column_count)]
    )
    pair_grad = lax.psum_scatter(
        every_grad.astype(jnp.bfloat16), "seq", scatter_dimension=1, tiled=True
    ).astype(jnp.float32)
    query_back = normalize_back(query_part, query_unit, query_inv)
    key_back = normalize_back(pair_grad[0].reshape(row_count, head_count, HD), key_unit, key_inv)
    qkv_low = jnp.concatenate(
        [
            query_back.reshape(row_count, column_count),
            key_back.reshape(row_count, column_count),
            pair_grad[1],
        ],
        axis=1,
    ).astype(jnp.bfloat16)
    inner_grad = jnp.einsum("rc,dc->rd", qkv_low, full_qkv, preferred_element_type=jnp.float32)
    attended_flat = attended_low.reshape(row_count, column_count)
    share_width = feature_count // lax.axis_size("tensor")
    own_share = summed_on_arrival(inner_grad.astype(jnp.bfloat16), "tensor", 1)
    offset = lax.axis_index("tensor") * share_width
    unit_own = lax.dynamic_slice_in_dim(normed, offset, share_width, 1)
    row_sums = in_one(
        (
            jnp.sum(own_share, axis=1, keepdims=True),
            jnp.sum(own_share * unit_own, axis=1, keepdims=True),
        ),
        "tensor",
    )
    branch = (
        own_share - row_sums[0] / feature_count - unit_own * (row_sums[1] / feature_count)
    ) * inverse
    left_rows = unit_low
    right_rows = grad_rows
    qkv_term = jnp.einsum(
        "rd,rc->dc", left_rows, qkv_low, preferred_element_type=jnp.float32
    ).reshape(lax.axis_size(("seq", "dp")) * own_rows, 3, column_count)
    out_term = jnp.einsum(
        "rd,rc->dc", right_rows, attended_flat, preferred_element_type=jnp.float32
    )
    summed = lax.psum_scatter(
        jnp.concatenate([qkv_term, out_term[:, None, :]], axis=1).astype(jnp.bfloat16),
        ("seq", "dp"),
        scatter_dimension=0,
        tiled=True,
    ).astype(jnp.float32)
    return (summed[:, :3], summed[:, 3], branch.astype(jnp.bfloat16)[None])


def solution(mesh):
    return jax.shard_map(
        local,
        mesh=mesh,
        in_specs=(
            P("dp", "seq", None),
            P("dp", "seq", None),
            P(("seq", "dp"), None, "tensor"),
            P(("seq", "dp"), "tensor"),
        ),
        out_specs=(
            P(("seq", "dp"), None, "tensor"),
            P(("seq", "dp"), "tensor"),
            P("dp", "seq", "tensor"),
        ),
        check_vma=False,
    )
```

profile of v0, /device:TPU:16, one launch (start us, length us, event | category | flops | bytes accessed | tf_op | source)
XLA Modules:
  0.0 414.2 jit_solution(13253095489150140398)
XLA Ops:
  12.4 73.2 %all-gather.3.cloned.1.call-done = bf16[3072,1536]{1,0:T(8,128)(2,1)} async-done(((bf16[96,1536]{1,0:T(8,128)(2,1)}), bf16[3072,1536]{1,0:T(8,128)(2,1)}) %all-gather.3.cloned.1.call-update) | async-done | bytes 9437200 | tf_op jit(solution)/shard_map/all_gather | solution.py:12
  85.5 5.3 %fusion.2 = f32[256,1152]{1,0:T(8,128)S(1)} fusion(bf16[3072,1536]{1,0:T(8,128)(2,1)} %all-gather.3.cloned.1.call-done, bf16[1,256,3072]{2,1,0:T(8,128)(2,1)S(1)} %copy-done.1, f32[256]{0:T(256)S(1)} %add_rsqrt_fusion.2, f32[256]{0:T(256)S(1)} %broadcast_multiply_fusion.6), kind=kOutput, calls=%fused_computation.5 | convolution fusion | flops 1815085056 | bytes 9832448 | tf_op jit(solution)/shard_map/dot_general | solution.py:76
  94.7 1.9 copy.92
  97.5 1.9 copy.91
  99.4 2.2 fusion.65
  104.7 3.2 fusion.38
  107.8 40.1 %all-gather.5.cloned.1.call-done = bf16[2,2048,384]{2,1,0:T(8,128)(2,1)} async-done(((bf16[2,256,384]{2,1,0:T(8,128)(2,1)}), bf16[2,2048,384]{2,1,0:T(8,128)(2,1)}) %all-gather.5.cloned.1.call-update) | async-done | bytes 3145744 | tf_op jit(solution)/shard_map/all_gather | solution.py:107
  147.9 3.9 fusion.64
  151.8 2.6 copy.93
  154.4 2.6 copy.97
  157.0 2.8 fusion.6
  159.8 2.6 fusion.22
  164.3 2.5 multiply_convert_fusion
  170.2 2.6 copy.100
  172.8 2.6 copy.101
  175.4 3.9 pad_maximum_fusion.1
  179.5 3.6 fusion.63
  185.7 3.4 fusion.7
  189.0 36.0 %reduce-scatter.3.cloned.1.call-done = bf16[2,256,384]{2,1,0:T(8,128)(2,1)} async-done(((bf16[2,2048,384]{2,1,0:T(8,128)(2,1)}), bf16[2,256,384]{2,1,0:T(8,128)(2,1)}) %reduce-scatter.3.cloned.1.call-update) | async-done | bytes 393232 | tf_op jit(solution)/shard_map/reduce_scatter | solution.py:141
  225.0 1.9 slice_convert_fusion.1
  226.9 1.9 copy.102
  232.7 1.9 copy.104
  236.8 1.9 fusion.53
  238.7 2.1 copy.107
  240.8 5.7 %convolution_convert_fusion = bf16[3072,3,384]{2,0,1:T(8,128)(2,1)} fusion(bf16[3,384,256]{2,1,0:T(8,128)(2,1)} %bitcast.114, bf16[1,256,3072]{2,1,0:T(8,128)(2,1)S(1)} %copy-done.1, f32[256]{0:T(256)S(1)} %copy-done.14, f32[256]{0:T(256)S(1)} %copy-done.12), kind=kOutput, calls=%fused_computation.7 | convolution fusion | flops 1818624000 | bytes 9242624 | tf_op jit(solution)/shard_map/rd,rc->dc/dot_general | solution.py:172
  246.5 8.4 %pad_maximum_fusion = bf16[3072,4,384]{2,0,1:T(8,128)(2,1)} fusion(bf16[3072,1,384]{2,0,1:T(8,128)(2,1)} %fusion.7, bf16[3072,3,384]{2,0,1:T(8,128)(2,1)} %convolution_convert_fusion), kind=kLoop, calls=%fused_computation | loop fusion | flops 4718592 | bytes 18874368 | tf_op jit(solution)/shard_map/concatenate | solution.py:179
  255.9 5.3 %fusion.8 = bf16[256,3072]{1,0:T(8,128)(2,1)S(1)} fusion(bf16[3072,1536]{1,0:T(8,128)(2,1)} %all-gather.3.cloned.1.call-done, bf16[256,384]{1,0:T(8,128)(2,1)} %get-tuple-element.14, bf16[256,384]{1,0:T(8,128)(2,1)S(1)} %copy-done.8, bf16[256,384]{1,0:T(8,128)(2,1)S(1)} %copy-done.9), kind=kOutput, calls=%fused_computation.18 | convolution fusion | flops 1814495232 | bytes 9240576 | tf_op jit(solution)/shard_map/rc,dc->rd/dot_general | solution.py:154
  262.6 7.3 %all-to-all-start = ((bf16[8,256,384]{2,1,0:T(8,128)(2,1)}), bf16[8,256,384]{2,1,0:T(8,128)(2,1)}, u32[]{:S(2)}, u32[]{:S(2)}) async-start(bf16[8,256,384]{2,1,0:T(8,128)(2,1)} %bitcast.107), calls=%async_computation.2 | async-start | bytes 3145728 | tf_op jit(solution)/shard_map/all_to_all | solution.py:26
  269.9 2.3 fusion.14
  272.2 17.6 %all-to-all-done = bf16[8,256,384]{2,1,0:T(8,128)(2,1)} async-done(((bf16[8,256,384]{2,1,0:T(8,128)(2,1)}), bf16[8,256,384]{2,1,0:T(8,128)(2,1)}, u32[]{:S(2)}, u32[]{:S(2)}) %all-to-all-start) | async-done | bytes 1572896 | tf_op jit(solution)/shard_map/all_to_all | solution.py:26
  292.8 12.0 %all_to_all.11 = f32[8,1,512]{2,1,0:T(1,128)S(1)} all-to-all(f32[8,1,512]{2,1,0:T(1,128)S(1)} %broadcast_in_dim.8), channel_id=1, replica_groups=mesh['seq'=8,'tensor'=8,'dp'=4] {'tensor'}, dimensions={0} | all-to-all | bytes 32768 | tf_op jit(solution)/shard_map/all_to_all | solution.py:32
  306.7 97.6 %reduce-scatter.5.cloned.1.call-done = bf16[96,4,384]{2,0,1:T(8,128)(2,1)} async-done(((bf16[3072,4,384]{2,0,1:T(8,128)(2,1)}), bf16[96,4,384]{2,0,1:T(8,128)(2,1)}) %reduce-scatter.5.cloned.1.call-update) | async-done | bytes 294928 | tf_op jit(solution)/shard_map/reduce_scatter | solution.py:178
  (81 shorter events, 37.5 us)
Async XLA Ops:
  7.2 97.5 %copy-start = (bf16[1,256,3072]{2,1,0:T(8,128)(2,1)S(1)}, bf16[1,256,3072]{2,1,0:T(8,128)(2,1)}, u32[]{:S(2)}) copy-start(bf16[1,256,3072]{2,1,0:T(8,128)(2,1)} %param.5) | copy-start | bytes 4718596
  7.2 4.6 %copy-start.1 = (bf16[1,256,3072]{2,1,0:T(8,128)(2,1)S(1)}, bf16[1,256,3072]{2,1,0:T(8,128)(2,1)}, u32[]{:S(2)}) copy-start(bf16[1,256,3072]{2,1,0:T(8,128)(2,1)} %param.4) | copy-start | bytes 4718596
  7.2 78.3 %all-gather.3.cloned.1.call-start = ((), (), s32[]{:S(2)}) async-start(), calls=%async_computation.4 | async-start | bytes 9732096 | tf_op jit(solution)/shard_map/all_gather | solution.py:12
  10.0 137.9 %all-gather.5.cloned.1.call-start = ((), (), s32[]{:S(2)}) async-start(), calls=%async_computation.5 | async-start | bytes 3538944 | tf_op jit(solution)/shard_map/all_gather | solution.py:107
  11.8 79.0 %copy-start.11 = (f32[256]{0:T(256)}, f32[256]{0:T(256)S(1)}, u32[]{:S(2)}) copy-start(f32[256]{0:T(256)S(1)} %broadcast_multiply_fusion.6) | copy-start | bytes 3076
  12.3 78.4 %copy-start.13 = (f32[256]{0:T(256)}, f32[256]{0:T(256)S(1)}, u32[]{:S(2)}) copy-start(f32[256]{0:T(256)S(1)} %add_rsqrt_fusion.2) | copy-start | bytes 3076
  90.8 1.2 copy-start.6
  93.8 9.5 %copy-start.4 = (f32[256,384]{0,1:T(8,128)}, f32[256,384]{0,1:T(8,128)S(1)}, u32[]{:S(2)}) copy-start(f32[256,384]{0,1:T(8,128)S(1)} %copy.90) | copy-start | bytes 1179652
  103.3 121.7 %reduce-scatter.3.cloned.1.call-start = ((), (), s32[]{:S(2)}) async-start(), calls=%async_computation.6 | async-start | bytes 3538944 | tf_op jit(solution)/shard_map/reduce_scatter | solution.py:141
  157.0 2.8 copy-start.10
  159.8 2.6 copy-start.3
  166.8 1.6 copy-start.2
  179.3 225.0 %reduce-scatter.5.cloned.1.call-start = ((), (), s32[]{:S(2)}) async-start(), calls=%async_computation.7 | async-start | bytes 9732096 | tf_op jit(solution)/shard_map/reduce_scatter | solution.py:178
  183.9 44.9 %copy-start.5 = (f32[256,384]{0,1:T(8,128)S(1)}, f32[256,384]{0,1:T(8,128)}, u32[]{:S(2)}) copy-start(f32[256,384]{0,1:T(8,128)} %copy-done.4) | copy-start | bytes 1179652
  231.9 8.9 %copy-start.12 = (f32[256]{0:T(256)S(1)}, f32[256]{0:T(256)}, u32[]{:S(2)}) copy-start(f32[256]{0:T(256)} %copy-done.11) | copy-start | bytes 3076
  231.9 8.9 %copy-start.14 = (f32[256]{0:T(256)S(1)}, f32[256]{0:T(256)}, u32[]{:S(2)}) copy-start(f32[256]{0:T(256)} %copy-done.13) | copy-start | bytes 3076
  236.1 0.7 copy-start.7
  254.9 0.9 copy-start.8
  254.9 1.0 copy-start.9
  262.6 27.2 %all-to-all-start = ((bf16[8,256,384]{2,1,0:T(8,128)(2,1)}), bf16[8,256,384]{2,1,0:T(8,128)(2,1)}, u32[]{:S(2)}, u32[]{:S(2)}) async-start(bf16[8,256,384]{2,1,0:T(8,128)(2,1)} %bitcast.107), calls=%async_computation.2 | async-start | bytes 3145728 | tf_op jit(solution)/shard_map/all_to_all | solution.py:26
Sparse Core Ops, SparseCore 0:
  10.4 75.0 all-gather.2
  103.4 44.4 all-gather.4
  179.4 45.5 reduce-scatter.2
  255.1 149.1 reduce-scatter.4
where the time goes:
time: 415 us; the launch traced here: 414 us
  waiting for transfers between devices  264 us (64%)
  local copies, waits for them, and re-layouts  42.5 us (10%)
  matrix products  37.9 us (9%)
  other arithmetic  35.6 us (9%)
  between operations  14 us (3%)
  blocking collectives  12 us (3%)
  starting transfers between devices  7.64 us (2%)
    reduce_scatter x1, waiting for transfers between devices, local(): lax.psum_scatter(jnp.concatenate([qkv_term, out_term[:, None, :]], axis=1...  97.6 us
    all_gather x1, waiting for transfers between devices, sent_together(): result, at, done = (lax.all_gather(both, axis, axis=dim, tiled=True), 0, [])  73.2 us
    all_gather x1, waiting for transfers between devices, local(): every_pair = lax.all_gather(key_value, 'seq', axis=1, tiled=True)  40.1 us
    reduce_scatter x1, waiting for transfers between devices, local(): lax.psum_scatter(every_grad.astype(jnp.bfloat16), 'seq', scatter_dimensio...  36 us
    all_to_all x1, waiting for transfers between devices, summed_on_arrival(): pieces = lax.all_to_all(split_up(shard, dim, size), axis, 0, 0, tiled=True)  17.6 us
    all_to_all x1, blocking collectives, copy_for_each(): return lax.all_to_all(copies, axis, split_axis=0, concat_axis=0, tiled=True)  12 us
    concatenate x1, other arithmetic, local(): jnp.concatenate([qkv_term, out_term[:, None, :]], axis=1)  8.45 us
  transfers between devices with their start and end apart: 5, of which 5 were waited for; matrix products, arithmetic and copies ran while one was open for 7% of the time, Pallas kernels for 0%

commit v1 on v0

--- a/solution.py
+++ b/solution.py
@@ -104,7 +104,10 @@
             * score_scale
         )
 
-    every_pair = lax.all_gather(key_value, "seq", axis=1, tiled=True)
+    def post_the_routes_all(base_x, link_axis):
+        return jnp.concatenate(lax.all_gather(base_x, link_axis), axis=1)
+
+    every_pair = post_the_routes_all(key_value, "seq")
     piece_rows = every_pair.shape[1]
     exponent = jnp.exp(scores_of(every_pair[0]))
     add_exp_total = jnp.sum(exponent, axis=-1)

time: 415 us -> 423 us (1.019)
  local copies, waits for them, and re-layouts: 42.5 us -> 49.8 us
    another operation x0 -> x2, local copies, waits for them, and re-layouts: none -> 7.5 us  [the longest x1 3.76 us: local(): value_rows = every_pair[1].reshape(piece_rows, head_count, HD)]
    all_gather x0 -> x1, local copies, waits for them, and re-layouts: none -> 5.13 us  [post_the_routes_all(): return jnp.concatenate(lax.all_gather(base_x, link_axis), axis=1)]
where the time goes in v1:
time: 423 us; the launch traced here: 421 us
  waiting for transfers between devices  264 us (62%)
  local copies, waits for them, and re-layouts  49.8 us (12%)
  matrix products  37.9 us (9%)
  other arithmetic  35.6 us (8%)
  between operations  14 us (3%)
  blocking collectives  11.8 us (3%)
  starting transfers between devices  7.78 us (2%)
    reduce_scatter x1, waiting for transfers between devices, local(): lax.psum_scatter(jnp.concatenate([qkv_term, out_term[:, None, :]], axis=1...  97 us
    all_gather x1, waiting for transfers between devices, sent_together(): result, at, done = (lax.all_gather(both, axis, axis=dim, tiled=True), 0, [])  73.2 us
    all_gather x1, waiting for transfers between devices, post_the_routes_all(): return jnp.concatenate(lax.all_gather(base_x, link_axis), axis=1)  39.9 us
    reduce_scatter x1, waiting for transfers between devices, local(): lax.psum_scatter(every_grad.astype(jnp.bfloat16), 'seq', scatter_dimensio...  35.9 us
    all_to_all x1, waiting for transfers between devices, summed_on_arrival(): pieces = lax.all_to_all(split_up(shard, dim, size), axis, 0, 0, tiled=True)  17.9 us
    all_to_all x1, blocking collectives, copy_for_each(): return lax.all_to_all(copies, axis, split_axis=0, concat_axis=0, tiled=True)  11.8 us
  transfers between devices with their start and end apart: 5, of which 5 were waited for; matrix products, arithmetic and copies ran while one was open for 7% of the time, Pallas kernels for 0%

profile of v1, /device:TPU:16, one launch (start us, length us, event | category | flops | bytes accessed | tf_op | source)
XLA Modules:
  0.0 420.9 jit_solution(4001057362221535600)
XLA Ops:
  12.4 73.2 %all-gather.4.cloned.1.call-done = bf16[3072,1536]{1,0:T(8,128)(2,1)} async-done(((bf16[96,1536]{1,0:T(8,128)(2,1)}), bf16[3072,1536]{1,0:T(8,128)(2,1)}) %all-gather.4.cloned.1.call-update) | async-done | bytes 9437200 | tf_op jit(solution)/shard_map/all_gather | solution.py:12
  85.5 5.3 %fusion.2 = f32[256,1152]{1,0:T(8,128)S(1)} fusion(bf16[3072,1536]{1,0:T(8,128)(2,1)} %all-gather.4.cloned.1.call-done, bf16[1,256,3072]{2,1,0:T(8,128)(2,1)S(1)} %copy-done.1, f32[256]{0:T(256)S(1)} %add_rsqrt_fusion.2, f32[256]{0:T(256)S(1)} %broadcast_multiply_fusion.6), kind=kOutput, calls=%fused_computation.5 | convolution fusion | flops 1815085056 | bytes 9832448 | tf_op jit(solution)/shard_map/dot_general | solution.py:76
  94.7 1.9 copy.87
  97.5 1.9 copy.86
  99.4 2.2 fusion.65
  104.8 3.2 fusion.38
  108.0 39.9 %all-gather.6.cloned.1.call-done = bf16[16,256,384]{2,1,0:T(8,128)(2,1)} async-done(((bf16[2,256,384]{2,1,0:T(8,128)(2,1)}), bf16[16,256,384]{2,1,0:T(8,128)(2,1)}) %all-gather.6.cloned.1.call-update) | async-done | bytes 3145744 | tf_op jit(solution)/shard_map/all_gather | solution.py:108
  147.9 5.1 %copy.88 = bf16[8,2,256,384]{2,0,3,1:T(8,128)(2,1)} copy(bf16[8,2,256,384]{3,2,1,0:T(8,128)(2,1)} %bitcast.119) | data formatting | bytes 6291456 | tf_op jit(solution)/shard_map/all_gather | solution.py:108
  153.0 3.8 fusion.64
  156.8 3.7 reshape_squeeze.14
  160.5 3.8 reshape_squeeze.15
  164.3 2.8 fusion.6
  167.1 2.6 fusion.22
  171.5 2.5 multiply_convert_fusion
  177.4 2.6 copy.94
  180.1 2.6 copy.95
  182.6 3.9 pad_maximum_fusion.1
  186.8 3.6 fusion.63
  193.0 3.4 fusion.7
  196.4 35.9 %reduce-scatter.3.cloned.1.call-done = bf16[2,256,384]{2,1,0:T(8,128)(2,1)} async-done(((bf16[2,2048,384]{2,1,0:T(8,128)(2,1)}), bf16[2,256,384]{2,1,0:T(8,128)(2,1)}) %reduce-scatter.3.cloned.1.call-update) | async-done | bytes 393232 | tf_op jit(solution)/shard_map/reduce_scatter | solution.py:144
  232.3 1.9 slice_convert_fusion.1
  234.2 1.9 copy.96
  239.9 1.9 copy.98
  246.0 2.1 copy.101
  248.1 5.7 %convolution_convert_fusion = bf16[3072,3,384]{2,0,1:T(8,128)(2,1)} fusion(bf16[3,384,256]{2,1,0:T(8,128)(2,1)} %bitcast.120, bf16[1,256,3072]{2,1,0:T(8,128)(2,1)S(1)} %copy-done.1, f32[256]{0:T(256)S(1)} %copy-done.14, f32[256]{0:T(256)S(1)} %copy-done.12), kind=kOutput, calls=%fused_computation.7 | convolution fusion | flops 1818624000 | bytes 9242624 | tf_op jit(solution)/shard_map/rd,rc->dc/dot_general | solution.py:175
  253.7 8.4 %pad_maximum_fusion = bf16[3072,4,384]{2,0,1:T(8,128)(2,1)} fusion(bf16[3072,1,384]{2,0,1:T(8,128)(2,1)} %fusion.7, bf16[3072,3,384]{2,0,1:T(8,128)(2,1)} %convolution_convert_fusion), kind=kLoop, calls=%fused_computation | loop fusion | flops 4718592 | bytes 18874368 | tf_op jit(solution)/shard_map/concatenate | solution.py:182
  263.2 5.3 %fusion.8 = bf16[256,3072]{1,0:T(8,128)(2,1)S(1)} fusion(bf16[3072,1536]{1,0:T(8,128)(2,1)} %all-gather.4.cloned.1.call-done, bf16[256,384]{1,0:T(8,128)(2,1)} %get-tuple-element.14, bf16[256,384]{1,0:T(8,128)(2,1)S(1)} %copy-done.8, bf16[256,384]{1,0:T(8,128)(2,1)S(1)} %copy-done.9), kind=kOutput, calls=%fused_computation.18 | convolution fusion | flops 1814495232 | bytes 9240576 | tf_op jit(solution)/shard_map/rc,dc->rd/dot_general | solution.py:157
  269.9 7.2 %all-to-all-start = ((bf16[8,256,384]{2,1,0:T(8,128)(2,1)}), bf16[8,256,384]{2,1,0:T(8,128)(2,1)}, u32[]{:S(2)}, u32[]{:S(2)}) async-start(bf16[8,256,384]{2,1,0:T(8,128)(2,1)} %bitcast.114), calls=%async_computation.2 | async-start | bytes 3145728 | tf_op jit(solution)/shard_map/all_to_all | solution.py:26
  277.1 2.3 fusion.14
  279.4 17.9 %all-to-all-done = bf16[8,256,384]{2,1,0:T(8,128)(2,1)} async-done(((bf16[8,256,384]{2,1,0:T(8,128)(2,1)}), bf16[8,256,384]{2,1,0:T(8,128)(2,1)}, u32[]{:S(2)}, u32[]{:S(2)}) %all-to-all-start) | async-done | bytes 1572896 | tf_op jit(solution)/shard_map/all_to_all | solution.py:26
  300.2 11.8 %all_to_all.11 = f32[8,1,512]{2,1,0:T(1,128)S(1)} all-to-all(f32[8,1,512]{2,1,0:T(1,128)S(1)} %broadcast_in_dim.8), channel_id=1, replica_groups=mesh['seq'=8,'tensor'=8,'dp'=4] {'tensor'}, dimensions={0} | all-to-all | bytes 32768 | tf_op jit(solution)/shard_map/all_to_all | solution.py:32
  313.9 97.0 %reduce-scatter.5.cloned.1.call-done = bf16[96,4,384]{2,0,1:T(8,128)(2,1)} async-done(((bf16[3072,4,384]{2,0,1:T(8,128)(2,1)}), bf16[96,4,384]{2,0,1:T(8,128)(2,1)}) %reduce-scatter.5.cloned.1.call-update) | async-done | bytes 294928 | tf_op jit(solution)/shard_map/reduce_scatter | solution.py:181
  (82 shorter events, 39.5 us)
Async XLA Ops:
  7.2 97.6 %copy-start = (bf16[1,256,3072]{2,1,0:T(8,128)(2,1)S(1)}, bf16[1,256,3072]{2,1,0:T(8,128)(2,1)}, u32[]{:S(2)}) copy-start(bf16[1,256,3072]{2,1,0:T(8,128)(2,1)} %param.5) | copy-start | bytes 4718596
  7.2 4.6 %copy-start.1 = (bf16[1,256,3072]{2,1,0:T(8,128)(2,1)S(1)}, bf16[1,256,3072]{2,1,0:T(8,128)(2,1)}, u32[]{:S(2)}) copy-start(bf16[1,256,3072]{2,1,0:T(8,128)(2,1)} %param.4) | copy-start | bytes 4718596
  7.2 78.3 %all-gather.4.cloned.1.call-start = ((), (), s32[]{:S(2)}) async-start(), calls=%async_computation.4 | async-start | bytes 9732096 | tf_op jit(solution)/shard_map/all_gather | solution.py:12
  10.0 137.9 %all-gather.6.cloned.1.call-start = ((), (), s32[]{:S(2)}) async-start(), calls=%async_computation.7 | async-start | bytes 3538944 | tf_op jit(solution)/shard_map/all_gather | solution.py:108
  11.8 79.0 %copy-start.11 = (f32[256]{0:T(256)}, f32[256]{0:T(256)S(1)}, u32[]{:S(2)}) copy-start(f32[256]{0:T(256)S(1)} %broadcast_multiply_fusion.6) | copy-start | bytes 3076
  12.3 78.4 %copy-start.13 = (f32[256]{0:T(256)}, f32[256]{0:T(256)S(1)}, u32[]{:S(2)}) copy-start(f32[256]{0:T(256)S(1)} %add_rsqrt_fusion.2) | copy-start | bytes 3076
  90.8 1.2 copy-start.6
  93.8 9.4 %copy-start.4 = (f32[256,384]{0,1:T(8,128)}, f32[256,384]{0,1:T(8,128)S(1)}, u32[]{:S(2)}) copy-start(f32[256,384]{0,1:T(8,128)S(1)} %copy.85) | copy-start | bytes 1179652
  103.3 129.0 %reduce-scatter.3.cloned.1.call-start = ((), (), s32[]{:S(2)}) async-start(), calls=%async_computation.5 | async-start | bytes 3538944 | tf_op jit(solution)/shard_map/reduce_scatter | solution.py:144
  164.3 2.8 copy-start.10
  167.1 2.6 copy-start.3
  174.1 1.6 copy-start.2
  186.6 224.4 %reduce-scatter.5.cloned.1.call-start = ((), (), s32[]{:S(2)}) async-start(), calls=%async_computation.6 | async-start | bytes 9732096 | tf_op jit(solution)/shard_map/reduce_scatter | solution.py:181
  191.2 44.9 %copy-start.5 = (f32[256,384]{0,1:T(8,128)S(1)}, f32[256,384]{0,1:T(8,128)}, u32[]{:S(2)}) copy-start(f32[256,384]{0,1:T(8,128)} %copy-done.4) | copy-start | bytes 1179652
  239.1 8.9 %copy-start.12 = (f32[256]{0:T(256)S(1)}, f32[256]{0:T(256)}, u32[]{:S(2)}) copy-start(f32[256]{0:T(256)} %copy-done.11) | copy-start | bytes 3076
  239.1 8.9 %copy-start.14 = (f32[256]{0:T(256)S(1)}, f32[256]{0:T(256)}, u32[]{:S(2)}) copy-start(f32[256]{0:T(256)} %copy-done.13) | copy-start | bytes 3076
  243.4 0.7 copy-start.7
  262.2 0.9 copy-start.8
  262.2 1.0 copy-start.9
  269.9 27.3 %all-to-all-start = ((bf16[8,256,384]{2,1,0:T(8,128)(2,1)}), bf16[8,256,384]{2,1,0:T(8,128)(2,1)}, u32[]{:S(2)}, u32[]{:S(2)}) async-start(bf16[8,256,384]{2,1,0:T(8,128)(2,1)} %bitcast.114), calls=%async_computation.2 | async-start | bytes 3145728 | tf_op jit(solution)/shard_map/all_to_all | solution.py:26
Sparse Core Ops, SparseCore 0:
  10.4 75.0 all-gather.3
  103.4 44.4 all-gather.5
  186.7 45.5 reduce-scatter.2
  262.3 148.5 reduce-scatter.4
